TPU v7x, 32 devices: a whole 2x2x4 slice. The times are simulated.
32 devices in a mesh: gx: 2 (over x), gy: 4 (over z), gz: 4 (over y, core).
Axes of the slice: x: 2, y: 2, z: 4, core: 2. Of those that a mesh axis runs over, the one named last changes fastest.
Arguments:
- acts: bfloat16 [40960, 768], P(('gx', 'gy', 'gz')), may hold values from -6 to 6
- grads_out: bfloat16 [40960, 768], P(('gx', 'gy', 'gz')), may hold values from -0.03125 to 0.03125
- master: float32 [4608, 128], P(('gx', 'gy', 'gz')), may hold values from -0.3 to 0.3
- moment: float32 [4608, 128], P(('gx', 'gy', 'gz')), may hold values from -6 to 6
- second: float32 [4608, 128], P(('gx', 'gy', 'gz')), may hold values from 0.1 to 2
Outputs:
- master_new: float32 [4608, 128], P(('gx', 'gy', 'gz'))
- moment_new: float32 [4608, 128], P(('gx', 'gy', 'gz'))
- second_new: float32 [4608, 128], P(('gx', 'gy', 'gz'))
- weights: bfloat16 [768, 768], replicated
All inputs are finite; a program needn't handle non-finite values.
Results may differ from a plain program's by a relative error of at most 0.003.
Values may be sent and summed in bfloat16 or wider, within the bound.
No kernel may reach another device: no remote copies, remote signals or barrier semaphores. Data moves between devices by JAX's collectives and lax.ppermute only.
A program may use at most 64 MiB of HBM per device.

v0:
```python
import jax
import jax.numpy as jnp
from jax import lax
from jax.sharding import PartitionSpec as P

STEP = 1000


def shards(acts, grads_out, master, moment, second):
    width_in = acts.shape[1]
    width_out = grads_out.shape[1]
    lane = master.shape[1]
    total_rows = width_in * width_out // lane
    local_grad = lax.dot_general(
        acts, grads_out, (((0,), (0,)), ((), ())), preferred_element_type=jnp.float32
    )
    local_flat = local_grad.reshape(total_rows, lane)
    partial_value = lax.psum_scatter(
        local_flat.astype(jnp.bfloat16), "gx", scatter_dimension=0, tiled=True
    ).astype(jnp.float32)
    partial_value = lax.psum_scatter(
        partial_value.astype(jnp.bfloat16), "gy", scatter_dimension=0, tiled=True
    ).astype(jnp.float32)
    gradient = lax.psum_scatter(
        partial_value.astype(jnp.bfloat16), "gz", scatter_dimension=0, tiled=True
    ).astype(jnp.float32)
    moment_new = 0.9 * moment + 0.1 * gradient
    second_new = 0.95 * second + 0.05 * gradient * gradient
    first_fix = 1.0 - 0.9**STEP
    second_fix = 1.0 - 0.95**STEP
    ratio = moment_new / first_fix / (jnp.sqrt(second_new / second_fix) + 1e-08)
    master_new = master - 0.01 * (ratio + 0.01 * master)
    rounded = master_new.astype(jnp.bfloat16)
    gathered = lax.all_gather(rounded, "gz", axis=0, tiled=True)
    gathered = lax.all_gather(gathered, "gy", axis=0, tiled=True)
    gathered = lax.all_gather(gathered, "gx", axis=0, tiled=True)
    weights = gathered.reshape(width_in, width_out)
    return (master_new, moment_new, second_new, weights)


def solution(mesh):
    return jax.shard_map(
        shards,
        mesh=mesh,
        in_specs=(
            P(("gx", "gy", "gz"), None),
            P(("gx", "gy", "gz"), None),
            P(("gx", "gy", "gz"), None),
            P(("gx", "gy", "gz"), None),
            P(("gx", "gy", "gz"), None),
        ),
        out_specs=(
            P(("gx", "gy", "gz"), None),
            P(("gx", "gy", "gz"), None),
            P(("gx", "gy", "gz"), None),
            P(),
        ),
        check_vma=False,
    )
```

profile of v0, /device:TPU:0, one launch (start us, length us, event | category | flops | bytes accessed | tf_op | source)
XLA Modules:
  0.0 141.0 jit_solution(13236243267090482629)
XLA Ops:
  7.2 0.0 copy-start
  7.2 0.0 reduce-scatter.4.cloned.1.call-start
  7.2 1.5 %copy-done = bf16[1280,768]{1,0:T(8,128)(2,1)S(1)} copy-done((bf16[1280,768]{1,0:T(8,128)(2,1)S(1)}, bf16[1280,768]{1,0:T(8,128)(2,1)}, u32[]{:S(2)}) %copy-start) | copy-done | bytes 1966104
  8.7 3.3 %convolution_convert_fusion = bf16[768,768]{1,0:T(8,128)(2,1)S(1)} fusion(bf16[1280,768]{1,0:T(8,128)(2,1)S(1)} %copy-done, bf16[1280,768]{1,0:T(8,128)(2,1)} %param.6), kind=kOutput, calls=%fused_computation | convolution fusion | flops 1510539264 | bytes 5111808 | tf_op jit(solution)/shard_map/dot_general | solution.py:14
  12.0 0.0 copy-start.1
  12.0 0.0 copy-start.2
  12.0 0.0 copy-start.3
  12.1 1.9 %convert_element_type.17 = bf16[4608,128]{1,0:T(8,128)(2,1)} reshape(bf16[768,768]{1,0:T(8,128)(2,1)S(1)} %convolution_convert_fusion) | data formatting | bytes 2359296 | tf_op jit(solution)/shard_map/convert_element_type | solution.py:19
  13.9 0.0 reduce-scatter.4.cloned.1.call-update
  13.9 0.0 reduce-scatter.6.cloned.1.call-start
  14.0 24.7 %reduce-scatter.4.cloned.1.call-done = bf16[2304,128]{1,0:T(8,128)(2,1)} async-done(((bf16[4608,128]{1,0:T(8,128)(2,1)}), bf16[2304,128]{1,0:T(8,128)(2,1)}) %reduce-scatter.4.cloned.1.call-update) | async-done | bytes 589840 | tf_op jit(solution)/shard_map/reduce_scatter | solution.py:18
  38.7 0.0 reduce-scatter.6.cloned.1.call-update
  38.7 0.0 reduce-scatter.8.cloned.1.call-start
  38.7 24.4 %reduce-scatter.6.cloned.1.call-done = bf16[576,128]{1,0:T(8,128)(2,1)} async-done(((bf16[2304,128]{1,0:T(8,128)(2,1)}), bf16[576,128]{1,0:T(8,128)(2,1)}) %reduce-scatter.6.cloned.1.call-update) | async-done | bytes 147472 | tf_op jit(solution)/shard_map/reduce_scatter | solution.py:21
  63.1 0.0 reduce-scatter.8.cloned.1.call-update
  63.1 0.0 all-gather.2.cloned.1.call-start
  63.2 20.5 %reduce-scatter.8.cloned.1.call-done = bf16[144,128]{1,0:T(8,128)(2,1)} async-done(((bf16[576,128]{1,0:T(8,128)(2,1)}), bf16[144,128]{1,0:T(8,128)(2,1)}) %reduce-scatter.8.cloned.1.call-update) | async-done | bytes 36880 | tf_op jit(solution)/shard_map/reduce_scatter | solution.py:24
  83.7 0.0 copy-done.1
  83.7 0.0 copy-done.2
  83.7 0.0 copy-done.3
  83.7 1.5 %fusion.2 = (bf16[144,128]{1,0:T(8,128)(2,1)S(1)}, f32[144,128]{1,0:T(8,128)}, f32[144,128]{1,0:T(8,128)}, f32[144,128]{1,0:T(8,128)}) fusion(f32[144,128]{1,0:T(8,128)S(1)} %copy-done.1, bf16[144,128]{1,0:T(8,128)(2,1)} %reduce-scatter.8.cloned.1.call-done, f32[144,128]{1,0:T(8,128)S(1)} %copy-done.2, f32[144,128]{1,0:T(8,128)S(1)} %copy-done.3), kind=kLoop, calls=%fused_computation.6 | loop fusion | flops 276480 | bytes 516096 | tf_op jit(solution)/shard_map/convert_element_type | solution.py:33
  85.2 5.4 %all_gather.9 = bf16[576,128]{1,0:T(8,128)(2,1)S(1)} all-gather(bf16[144,128]{1,0:T(8,128)(2,1)S(1)} %get-tuple-element.4), channel_id=1, replica_groups=mesh['gx'=2,'gy'=4,'gz'=4] {'gz'}, dimensions={0}, use_global_device_ids=true | all-gather | bytes 184320 | tf_op jit(solution)/shard_map/all_gather | solution.py:34
  90.6 17.2 %all_gather.10 = bf16[2304,128]{1,0:T(8,128)(2,1)} all-gather(bf16[576,128]{1,0:T(8,128)(2,1)S(1)} %all_gather.9), channel_id=1, replica_groups=mesh['gx'=2,'gy'=4,'gz'=4] {'gy'}, dimensions={0}, use_global_device_ids=true | all-gather | bytes 737280 | tf_op jit(solution)/shard_map/all_gather | solution.py:35
  107.8 0.0 all-gather.2.cloned.1.call-update
  107.8 23.3 %all-gather.2.cloned.1.call-done = bf16[4608,128]{1,0:T(8,128)(2,1)} async-done(((bf16[2304,128]{1,0:T(8,128)(2,1)}), bf16[4608,128]{1,0:T(8,128)(2,1)}) %all-gather.2.cloned.1.call-update) | async-done | bytes 1179664 | tf_op jit(solution)/shard_map/all_gather | solution.py:36
  131.1 3.3 %reshape.13 = bf16[768,768]{1,0:T(8,128)(2,1)} reshape(bf16[4608,128]{1,0:T(8,128)(2,1)} %all-gather.2.cloned.1.call-done) | data formatting | bytes 2359296 | tf_op jit(solution)/shard_map/reshape | solution.py:37
Async XLA Ops:
  7.2 1.6 %copy-start = (bf16[1280,768]{1,0:T(8,128)(2,1)S(1)}, bf16[1280,768]{1,0:T(8,128)(2,1)}, u32[]{:S(2)}) copy-start(bf16[1280,768]{1,0:T(8,128)(2,1)} %param.5) | copy-start | bytes 5898244
  7.2 31.5 %reduce-scatter.4.cloned.1.call-start = ((), (), s32[]{:S(2)}) async-start(), calls=%async_computation.3 | async-start | bytes 1769472 | tf_op jit(solution)/shard_map/reduce_scatter | solution.py:18
  12.0 71.7 %copy-start.1 = (f32[144,128]{1,0:T(8,128)S(1)}, f32[144,128]{1,0:T(8,128)}, u32[]{:S(2)}) copy-start(f32[144,128]{1,0:T(8,128)} %param.7) | copy-start | bytes 221188
  12.0 71.7 %copy-start.2 = (f32[144,128]{1,0:T(8,128)S(1)}, f32[144,128]{1,0:T(8,128)}, u32[]{:S(2)}) copy-start(f32[144,128]{1,0:T(8,128)} %param.9) | copy-start | bytes 221188
  12.0 71.7 %copy-start.3 = (f32[144,128]{1,0:T(8,128)S(1)}, f32[144,128]{1,0:T(8,128)}, u32[]{:S(2)}) copy-start(f32[144,128]{1,0:T(8,128)} %param.8) | copy-start | bytes 221188
  13.9 49.2 %reduce-scatter.6.cloned.1.call-start = ((), (), s32[]{:S(2)}) async-start(), calls=%async_computation.4 | async-start | bytes 737280 | tf_op jit(solution)/shard_map/reduce_scatter | solution.py:21
  38.7 45.0 %reduce-scatter.8.cloned.1.call-start = ((), (), s32[]{:S(2)}) async-start(), calls=%async_computation.5 | async-start | bytes 184320 | tf_op jit(solution)/shard_map/reduce_scatter | solution.py:24
  63.1 68.0 %all-gather.2.cloned.1.call-start = ((), (), s32[]{:S(2)}) async-start(), calls=%async_computation.6 | async-start | bytes 1769472 | tf_op jit(solution)/shard_map/all_gather | solution.py:36
Sparse Core Ops, SparseCore 0:
  14.1 24.5 reduce-scatter.3
  40.9 22.1 reduce-scatter.5
  65.5 18.1 reduce-scatter.7
  108.0 23.0 all-gather.1
where the time goes:
time: 141 us
  waiting for transfers between devices  92.9 us (66%)
  blocking collectives  22.6 us (16%)
  between operations  13.8 us (10%)
  local copies, waits for them, and re-layouts  6.73 us (5%)
  matrix products  3.29 us (2%)
  other arithmetic  1.48 us (1%)
    reduce_scatter x1, waiting for transfers between devices, shards(): lax.psum_scatter(local_flat.astype(jnp.bfloat16), 'gx', scatter_dimension...  24.7 us
    reduce_scatter x1, waiting for transfers between devices, shards(): lax.psum_scatter(partial_value.astype(jnp.bfloat16), 'gy', scatter_dimens...  24.4 us
    all_gather x1, waiting for transfers between devices, shards(): gathered = lax.all_gather(gathered, 'gx', axis=0, tiled=True)  23.3 us
    reduce_scatter x1, waiting for transfers between devices, shards(): lax.psum_scatter(partial_value.astype(jnp.bfloat16), 'gz', scatter_dimens...  20.5 us
    all_gather x1, blocking collectives, shards(): gathered = lax.all_gather(gathered, 'gy', axis=0, tiled=True)  17.2 us
    all_gather x1, blocking collectives, shards(): gathered = lax.all_gather(rounded, 'gz', axis=0, tiled=True)  5.45 us
    reshape x1, local copies, waits for them, and re-layouts, shards(): weights = gathered.reshape(width_in, width_out)  3.35 us
    dot_general x1, matrix products, shards(): lax.dot_general(acts, grads_out, (((0,), (0,)), ((), ())), preferred_elem...  3.29 us
  transfers between devices with their start and end apart: 4, of which 4 were waited for; matrix products, arithmetic and copies ran while one was open for 0% of the time, Pallas kernels for 0%

commit v1 on v0

--- a/solution.py
+++ b/solution.py
@@ -32,7 +32,12 @@
     master_new = master - 0.01 * (ratio + 0.01 * master)
     rounded = master_new.astype(jnp.bfloat16)
     gathered = lax.all_gather(rounded, "gz", axis=0, tiled=True)
-    gathered = lax.all_gather(gathered, "gy", axis=0, tiled=True)
+    ring = [gathered]
+    for hop in range(3):
+        ring.append(lax.ppermute(ring[-1], "gy", [(dev, (dev + 1) % 4) for dev in range(4)]))
+    gathered = jnp.roll(
+        jnp.concatenate(ring[::-1], axis=0), (lax.axis_index("gy") + 1) * ring[0].shape[0], axis=0
+    )
     gathered = lax.all_gather(gathered, "gx", axis=0, tiled=True)
     weights = gathered.reshape(width_in, width_out)
     return (master_new, moment_new, second_new, weights)

time: 141 us -> 144 us (1.021)
  blocking collectives: 22.6 us -> 5.45 us
  waiting for transfers between devices: 92.9 us -> 110 us
  starting transfers between devices: 0.16 us -> 1.64 us
    ppermute x0 -> x3, waiting for transfers between devices: none -> 20.4 us  [shards(): lax.ppermute(ring[-1], 'gy', [(dev, (dev + 1) % 4) for dev in range(4)])]
    all_gather x1 -> x0, blocking collectives: 17.2 us -> none  [shards(): gathered = lax.all_gather(gathered, 'gy', axis=0, tiled=True)]
    all_gather x1, waiting for transfers between devices: 23.3 us -> 20.2 us  [shards(): gathered = lax.all_gather(gathered, 'gx', axis=0, tiled=True)]
    ppermute x0 -> x3, starting transfers between devices: none -> 1.49 us  [shards(): lax.ppermute(ring[-1], 'gy', [(dev, (dev + 1) % 4) for dev in range(4)])]
  transfers between devices with their start and end apart: 4 -> 7, of which waited for: 4 -> 7; matrix products, arithmetic and copies ran while one was open for 0% -> 0% of each run, Pallas kernels for 0% -> 0%
where the time goes in v1:
time: 144 us
  waiting for transfers between devices  110 us (76%)
  between operations  13.8 us (10%)
  local copies, waits for them, and re-layouts  7.86 us (5%)
  blocking collectives  5.45 us (4%)
  matrix products  3.29 us (2%)
  starting transfers between devices  1.64 us (1%)
  other arithmetic  1.48 us (1%)
    reduce_scatter x1, waiting for transfers between devices, shards(): lax.psum_scatter(local_flat.astype(jnp.bfloat16), 'gx', scatter_dimension...  24.7 us
    reduce_scatter x1, waiting for transfers between devices, shards(): lax.psum_scatter(partial_value.astype(jnp.bfloat16), 'gy', scatter_dimens...  24.4 us
    reduce_scatter x1, waiting for transfers between devices, shards(): lax.psum_scatter(partial_value.astype(jnp.bfloat16), 'gz', scatter_dimens...  20.5 us
    ppermute x3, waiting for transfers between devices, shards(): lax.ppermute(ring[-1], 'gy', [(dev, (dev + 1) % 4) for dev in range(4)])  20.4 us
    all_gather x1, waiting for transfers between devices, shards(): gathered = lax.all_gather(gathered, 'gx', axis=0, tiled=True)  20.2 us
    all_gather x1, blocking collectives, shards(): gathered = lax.all_gather(rounded, 'gz', axis=0, tiled=True)  5.45 us
    reshape x1, local copies, waits for them, and re-layouts, shards(): weights = gathered.reshape(width_in, width_out)  3.35 us
    dot_general x1, matrix products, shards(): lax.dot_general(acts, grads_out, (((0,), (0,)), ((), ())), preferred_elem...  3.29 us
  transfers between devices with their start and end apart: 7, of which 7 were waited for; matrix products, arithmetic and copies ran while one was open for 0% of the time, Pallas kernels for 0%

profile of v1, /device:TPU:0, one launch (start us, length us, event | category | flops | bytes accessed | tf_op | source)
XLA Modules:
  0.0 143.7 jit_solution(3440438258364149620)
XLA Ops:
  7.2 0.0 copy-start
  7.2 0.0 reduce-scatter.4.cloned.1.call-start
  7.2 1.5 %copy-done = bf16[1280,768]{1,0:T(8,128)(2,1)S(1)} copy-done((bf16[1280,768]{1,0:T(8,128)(2,1)S(1)}, bf16[1280,768]{1,0:T(8,128)(2,1)}, u32[]{:S(2)}) %copy-start) | copy-done | bytes 1966104
  8.7 3.3 %convolution_convert_fusion = bf16[768,768]{1,0:T(8,128)(2,1)S(1)} fusion(bf16[1280,768]{1,0:T(8,128)(2,1)S(1)} %copy-done, bf16[1280,768]{1,0:T(8,128)(2,1)} %param.6), kind=kOutput, calls=%fused_computation | convolution fusion | flops 1510539264 | bytes 5111808 | tf_op jit(solution)/shard_map/dot_general | solution.py:14
  12.0 1.9 %convert_element_type.17 = bf16[4608,128]{1,0:T(8,128)(2,1)} reshape(bf16[768,768]{1,0:T(8,128)(2,1)S(1)} %convolution_convert_fusion) | data formatting | bytes 2359296 | tf_op jit(solution)/shard_map/convert_element_type | solution.py:19
  13.9 0.0 copy-start.1
  13.9 0.0 copy-start.2
  13.9 0.0 copy-start.3
  13.9 0.0 reduce-scatter.4.cloned.1.call-update
  13.9 0.0 reduce-scatter.6.cloned.1.call-start
  14.0 24.7 %reduce-scatter.4.cloned.1.call-done = bf16[2304,128]{1,0:T(8,128)(2,1)} async-done(((bf16[4608,128]{1,0:T(8,128)(2,1)}), bf16[2304,128]{1,0:T(8,128)(2,1)}) %reduce-scatter.4.cloned.1.call-update) | async-done | bytes 589840 | tf_op jit(solution)/shard_map/reduce_scatter | solution.py:18
  38.6 0.0 reduce-scatter.6.cloned.1.call-update
  38.6 0.0 reduce-scatter.8.cloned.1.call-start
  38.7 24.4 %reduce-scatter.6.cloned.1.call-done = bf16[576,128]{1,0:T(8,128)(2,1)} async-done(((bf16[2304,128]{1,0:T(8,128)(2,1)}), bf16[576,128]{1,0:T(8,128)(2,1)}) %reduce-scatter.6.cloned.1.call-update) | async-done | bytes 147472 | tf_op jit(solution)/shard_map/reduce_scatter | solution.py:21
  63.1 0.0 reduce-scatter.8.cloned.1.call-update
  63.1 0.0 all-gather.2.cloned.1.call-start
  63.1 20.5 %reduce-scatter.8.cloned.1.call-done = bf16[144,128]{1,0:T(8,128)(2,1)} async-done(((bf16[576,128]{1,0:T(8,128)(2,1)}), bf16[144,128]{1,0:T(8,128)(2,1)}) %reduce-scatter.8.cloned.1.call-update) | async-done | bytes 36880 | tf_op jit(solution)/shard_map/reduce_scatter | solution.py:24
  83.7 0.0 copy-done.1
  83.7 0.0 copy-done.2
  83.7 0.0 copy-done.3
  83.7 1.5 %fusion.2 = (bf16[144,128]{1,0:T(8,128)(2,1)S(1)}, f32[144,128]{1,0:T(8,128)}, f32[144,128]{1,0:T(8,128)}, f32[144,128]{1,0:T(8,128)}) fusion(f32[144,128]{1,0:T(8,128)S(1)} %copy-done.1, bf16[144,128]{1,0:T(8,128)(2,1)} %reduce-scatter.8.cloned.1.call-done, f32[144,128]{1,0:T(8,128)S(1)} %copy-done.2, f32[144,128]{1,0:T(8,128)S(1)} %copy-done.3), kind=kLoop, calls=%fused_computation.15 | loop fusion | flops 276480 | bytes 516096 | tf_op jit(solution)/shard_map/convert_element_type | solution.py:33
  85.1 5.4 %all_gather.6 = bf16[576,128]{1,0:T(8,128)(2,1)S(1)} all-gather(bf16[144,128]{1,0:T(8,128)(2,1)S(1)} %get-tuple-element.4), channel_id=1, replica_groups=mesh['gx'=2,'gy'=4,'gz'=4] {'gz'}, dimensions={0}, use_global_device_ids=true | all-gather | bytes 184320 | tf_op jit(solution)/shard_map/all_gather | solution.py:34
  90.6 1.5 %collective-permute-start = (bf16[576,128]{1,0:T(8,128)(2,1)S(1)}, bf16[576,128]{1,0:T(8,128)(2,1)S(1)}, u32[]{:S(2)}, u32[]{:S(2)}) collective-permute-start(bf16[576,128]{1,0:T(8,128)(2,1)S(1)} %all_gather.6), channel_id=1, source_target_pairs={{0,4},{4,8},{8,12},{12,0},{1,5},{5,9},{9,13},{13,1},{2,6},{6,10},{... | collective-permute-start | bytes 442376 | tf_op jit(solution)/shard_map/ppermute | solution.py:37
  92.1 6.4 %collective-permute-done = bf16[576,128]{1,0:T(8,128)(2,1)S(1)} collective-permute-done((bf16[576,128]{1,0:T(8,128)(2,1)S(1)}, bf16[576,128]{1,0:T(8,128)(2,1)S(1)}, u32[]{:S(2)}, u32[]{:S(2)}) %collective-permute-start) | collective-permute-done | bytes 147488 | tf_op jit(solution)/shard_map/ppermute | solution.py:37
  98.5 0.0 collective-permute-start.1
  98.5 7.0 %collective-permute-done.1 = bf16[576,128]{1,0:T(8,128)(2,1)S(1)} collective-permute-done((bf16[576,128]{1,0:T(8,128)(2,1)S(1)}, bf16[576,128]{1,0:T(8,128)(2,1)S(1)}, u32[]{:S(2)}, u32[]{:S(2)}) %collective-permute-start.1) | collective-permute-done | bytes 147488 | tf_op jit(solution)/shard_map/ppermute | solution.py:37
  105.5 0.0 collective-permute-start.2
  105.5 6.9 %collective-permute-done.2 = bf16[576,128]{1,0:T(8,128)(2,1)S(1)} collective-permute-done((bf16[576,128]{1,0:T(8,128)(2,1)S(1)}, bf16[576,128]{1,0:T(8,128)(2,1)S(1)}, u32[]{:S(2)}, u32[]{:S(2)}) %collective-permute-start.2) | collective-permute-done | bytes 147488 | tf_op jit(solution)/shard_map/ppermute | solution.py:37
  112.7 1.0 constant_dynamic-slice_fusion
  113.7 0.0 all-gather.2.cloned.1.call-update
  113.7 20.2 %all-gather.2.cloned.1.call-done = bf16[4608,128]{1,0:T(8,128)(2,1)} async-done(((bf16[2304,128]{1,0:T(8,128)(2,1)}), bf16[4608,128]{1,0:T(8,128)(2,1)}) %all-gather.2.cloned.1.call-update) | async-done | bytes 1179664 | tf_op jit(solution)/shard_map/all_gather | solution.py:41
  133.8 3.3 %reshape.13 = bf16[768,768]{1,0:T(8,128)(2,1)} reshape(bf16[4608,128]{1,0:T(8,128)(2,1)} %all-gather.2.cloned.1.call-done) | data formatting | bytes 2359296 | tf_op jit(solution)/shard_map/reshape | solution.py:42
  (8 shorter events, 0.2 us)
Async XLA Ops:
  7.2 1.6 %copy-start = (bf16[1280,768]{1,0:T(8,128)(2,1)S(1)}, bf16[1280,768]{1,0:T(8,128)(2,1)}, u32[]{:S(2)}) copy-start(bf16[1280,768]{1,0:T(8,128)(2,1)} %param.5) | copy-start | bytes 5898244
  7.2 31.4 %reduce-scatter.4.cloned.1.call-start = ((), (), s32[]{:S(2)}) async-start(), calls=%async_computation.3 | async-start | bytes 1769472 | tf_op jit(solution)/shard_map/reduce_scatter | solution.py:18
  13.9 69.8 %copy-start.1 = (f32[144,128]{1,0:T(8,128)S(1)}, f32[144,128]{1,0:T(8,128)}, u32[]{:S(2)}) copy-start(f32[144,128]{1,0:T(8,128)} %param.7) | copy-start | bytes 221188
  13.9 69.8 %copy-start.2 = (f32[144,128]{1,0:T(8,128)S(1)}, f32[144,128]{1,0:T(8,128)}, u32[]{:S(2)}) copy-start(f32[144,128]{1,0:T(8,128)} %param.9) | copy-start | bytes 221188
  13.9 69.8 %copy-start.3 = (f32[144,128]{1,0:T(8,128)S(1)}, f32[144,128]{1,0:T(8,128)}, u32[]{:S(2)}) copy-start(f32[144,128]{1,0:T(8,128)} %param.8) | copy-start | bytes 221188
  13.9 49.2 %reduce-scatter.6.cloned.1.call-start = ((), (), s32[]{:S(2)}) async-start(), calls=%async_computation.4 | async-start | bytes 737280 | tf_op jit(solution)/shard_map/reduce_scatter | solution.py:21
  38.6 45.0 %reduce-scatter.8.cloned.1.call-start = ((), (), s32[]{:S(2)}) async-start(), calls=%async_computation.5 | async-start | bytes 184320 | tf_op jit(solution)/shard_map/reduce_scatter | solution.py:24
  63.1 70.7 %all-gather.2.cloned.1.call-start = ((), (), s32[]{:S(2)}) async-start(), calls=%async_computation.6 | async-start | bytes 1769472 | tf_op jit(solution)/shard_map/all_gather | solution.py:41
  90.6 7.9 %collective-permute-start = (bf16[576,128]{1,0:T(8,128)(2,1)S(1)}, bf16[576,128]{1,0:T(8,128)(2,1)S(1)}, u32[]{:S(2)}, u32[]{:S(2)}) collective-permute-start(bf16[576,128]{1,0:T(8,128)(2,1)S(1)} %all_gather.6), channel_id=1, source_target_pairs={{0,4},{4,8},{8,12},{12,0},{1,5},{5,9},{9,13},{13,1},{2,6},{6,10},{... | collective-permute-start | bytes 442376 | tf_op jit(solution)/shard_map/ppermute | solution.py:37
  98.5 7.0 %collective-permute-start.1 = (bf16[576,128]{1,0:T(8,128)(2,1)S(1)}, bf16[576,128]{1,0:T(8,128)(2,1)S(1)}, u32[]{:S(2)}, u32[]{:S(2)}) collective-permute-start(bf16[576,128]{1,0:T(8,128)(2,1)S(1)} %collective-permute-done), channel_id=1, source_target_pairs={{0,4},{4,8},{8,12},{12,0},{1,5},{5,9},{9,13},{13,1},{2,6},{6,10},{... | collective-permute-start | bytes 442376 | tf_op jit(solution)/shard_map/ppermute | solution.py:37
  105.5 6.9 %collective-permute-start.2 = (bf16[576,128]{1,0:T(8,128)(2,1)S(1)}, bf16[576,128]{1,0:T(8,128)(2,1)S(1)}, u32[]{:S(2)}, u32[]{:S(2)}) collective-permute-start(bf16[576,128]{1,0:T(8,128)(2,1)S(1)} %collective-permute-done.1), channel_id=1, source_target_pairs={{0,4},{4,8},{8,12},{12,0},{1,5},{5,9},{9,13},{13,1},{2,6},{6,10},{... | collective-permute-start | bytes 442376 | tf_op jit(solution)/shard_map/ppermute | solution.py:37
Sparse Core Ops, SparseCore 0:
  14.0 24.5 reduce-scatter.3
  40.9 22.1 reduce-scatter.5
  65.5 18.1 reduce-scatter.7
  113.8 19.9 all-gather.1
